TPU v7x, 32 devices: a whole 2x2x4 slice. The times are simulated.
32 devices in a mesh: groups: 2 (over x), tile: 16 (over z, y, core).
Axes of the slice: x: 2, y: 2, z: 4, core: 2. Of those that a mesh axis runs over, the one named last changes fastest.
Arguments:
- self_query: bfloat16 [4096, 4096], P(('groups', 'tile')), parts along dimension 0, may hold values from -110 to 110
- self_key: bfloat16 [4096, 4096], P(('groups', 'tile')), parts along dimension 0, may hold values from -6 to 6
- self_value: bfloat16 [4096, 4096], P(('groups', 'tile')), parts along dimension 0, may hold values from -24 to 24
- cross_query: bfloat16 [4096, 4096], P(('groups', 'tile')), parts along dimension 0, may hold values from -110 to 110
- text_key: bfloat16 [512, 4096], P(('groups', 'tile')), parts along dimension 0, may hold values from -6 to 6
- text_value: bfloat16 [512, 4096], P(('groups', 'tile')), parts along dimension 0, may hold values from -24 to 24
- timestep: int32 [1], replicated, may hold values from 0 to 49
- gate_table: bfloat16 [50, 4096], replicated, may hold values from 0.5 to 2
Outputs:
- mixed: bfloat16 [4096, 4096], P(('groups', 'tile')), parts along dimension 0
There are 2 independent parts, one for each index of `groups`. A program takes and returns all parts, laid end to end along the dimension named above; an argument that names none is the same for every part. Nothing has to cross between parts.
All inputs are finite; a program needn't handle non-finite values.
Results may differ from a plain program's by a relative error of at most 0.0032.
Values may be sent and summed in bfloat16 or wider, within the bound.
A program may use at most 64 MiB of HBM per device.

v0:
```python
import functools
import math

import jax
import jax.numpy as jnp
from jax import lax
from jax.experimental import pallas as pl
from jax.experimental.pallas import tpu as pltpu
from jax.sharding import PartitionSpec as P

HEADS = 32
RADIUS = 2
GROUPS = 8
AHEAD = 8
LAG = 3
TEXT_GAP = 1
SCORE_ROUND = 7
EARLY_HEADS = 32
UNROLL = 4
MESH = pl.DeviceIdType.MESH
OWN, PARTNER, NEAR, DIAG, FAR = range(5)


def softmax_parts(scores, scale):
    top = scores[0]
    for block in scores[1:]:
        top = jnp.maximum(top, block)
    top = jnp.max(top, axis=1, keepdims=True)
    weights = [jnp.exp2((block - top) * scale) for block in scores]
    total = weights[0]
    for block in weights[1:]:
        total = total + block
    total = jnp.sum(total, axis=1, keepdims=True)
    rounded = jnp.concatenate([block.astype(jnp.bfloat16) for block in weights], axis=1)
    return rounded, total


def scores_of(query, keys):
    return lax.dot_general(query, keys, (((1,), (1,)), ((), ())), preferred_element_type=jnp.float32)


def kernel(
    tiles, relay_text, step_ref, q_hbm, k_hbm, v_hbm, cq_hbm, tk_hbm, tv_hbm, gate_hbm, out_ref,
    q_ref, cq_ref, gate_ref, kbuf, vbuf, tkbuf, tvbuf, self_acc, cross_acc, weight_ref,
    local_sem, own_sem, near_send, near_recv, relay_send, far_recv, part_send, part_recv, diag_send, diag_recv,
    half_send, half_recv, pair_send, pair_recv, share_send, share_recv, across_send,
):
    tokens, width = q_ref.shape
    head_dim = width // HEADS
    columns = width // GROUPS
    heads = HEADS // GROUPS
    depth = tiles // 4
    text_rows = tk_hbm.shape[0]

    t = lax.axis_index("tile")
    core = lax.rem(t, 2)
    side = lax.rem(t // 2, 2)
    place = t // 4
    partner = t + 1 - 2 * core
    buddy = t + 2 - 4 * side
    ahead = t + 4 - 8 * side
    behind = t - 4 + 8 * side
    has_ahead = (ahead >= 0) & (ahead < tiles)
    has_far = (behind >= 0) & (behind < tiles)
    has_up = place < depth - 1
    has_down = place > 0
    gives_near = side == core
    has_diag = has_far | (side != core)

    def remote(src, dst, send, recv, device):
        return pltpu.make_async_remote_copy(
            src_ref=src, dst_ref=dst, send_sem=send, recv_sem=recv, device_id={"tile": device}, device_id_type=MESH
        )

    def cols(g):
        return pl.ds(pl.multiple_of(g * columns, columns), columns)

    sources = (k_hbm, v_hbm)
    buffers = (kbuf, vbuf)
    texts = (tk_hbm, tv_hbm)
    text_buffers = (tkbuf, tvbuf)

    def local_copies():
        copies = [
            pltpu.make_async_copy(q_hbm, q_ref, local_sem.at[0]),
            pltpu.make_async_copy(cq_hbm, cq_ref, local_sem.at[1]),
            pltpu.make_async_copy(gate_hbm, gate_ref, local_sem.at[4]),
        ]
        for i in range(2):
            copies.append(pltpu.make_async_copy(sources[i], buffers[i].at[OWN], own_sem.at[i]))
        if relay_text:
            row = ((place * 2 + core) * 2 + side) * text_rows
            for i in range(2):
                copies.append(
                    pltpu.make_async_copy(
                        texts[i],
                        text_buffers[i].at[pl.ds(pl.multiple_of(row, text_rows), text_rows), :],
                        local_sem.at[2 + i],
                    )
                )
        else:
            for i in range(2):
                copies.append(pltpu.make_async_copy(texts[i], text_buffers[i], local_sem.at[2 + i]))
        return copies

    for copy in local_copies():
        copy.start()

    barrier = pltpu.get_barrier_semaphore()

    def greet(device):
        pl.semaphore_signal(barrier, inc=1, device_id={"tile": device}, device_id_type=MESH)

    greet(partner)
    greet(buddy)

    @pl.when(has_up)
    def _():
        greet(t + 4)

    @pl.when(has_down)
    def _():
        greet(t - 4)

    pl.semaphore_wait(barrier, 2 + has_up.astype(jnp.int32) + has_down.astype(jnp.int32))

    def near_copy(g, i):
        return remote(
            sources[i].at[:, cols(g)], buffers[i].at[NEAR, :, cols(g)], near_send.at[g, i], near_recv.at[g, i], buddy
        )

    def part_copy(g, i):
        return remote(
            sources[i].at[:, cols(g)], buffers[i].at[PARTNER, :, cols(g)], part_send.at[g, i], part_recv.at[g, i], partner
        )

    def relay_copy(g, i):
        return remote(
            buffers[i].at[NEAR, :, cols(g)], buffers[i].at[FAR, :, cols(g)], relay_send.at[g, i], far_recv.at[g, i], ahead
        )

    def far_copy(g, i):
        return remote(
            buffers[i].at[NEAR, :, cols(g)], buffers[i].at[FAR, :, cols(g)], relay_send.at[g, i], far_recv.at[g, i], behind
        )

    def diag_copy(g, i, slot):
        return remote(
            buffers[i].at[slot, :, cols(g)], buffers[i].at[DIAG, :, cols(g)], diag_send.at[g, i], diag_recv.at[g, i], partner
        )

    early = EARLY_HEADS * head_dim
    pieces = ((0, 0, early, False), (1, 0, width, True))
    if early < width:
        pieces += ((0, early, width - early, True),)
    late = range(1, len(pieces))

    def text_part(n, rows):
        i, first, count, _ = pieces[n]
        return text_buffers[i].at[rows, pl.ds(first, count)]

    def half_rows(which):
        row = ((place * 2 + core) * 2 + which) * text_rows
        return pl.ds(pl.multiple_of(row, text_rows), text_rows)

    def pair_rows(where, which):
        row = (where * 2 + which) * 2 * text_rows
        return pl.ds(pl.multiple_of(row, 2 * text_rows), 2 * text_rows)

    def half_copy(i, which):
        return remote(texts[i], text_buffers[i].at[half_rows(which), :], half_send.at[i], half_recv.at[i], buddy)

    def chain_copy(where, i, up):
        part = text_part(i, pair_rows(where, core))
        return remote(part, part, pair_send.at[where, i, int(up)], pair_recv.at[where, i], t + (4 if up else -4))

    def across_copy(where, i):
        part = text_part(i, pair_rows(where, core))
        return remote(part, part, across_send.at[where, i], pair_recv.at[where, i], buddy)

    def share_copy(where, i, which):
        part = text_part(i, pair_rows(where, which))
        return remote(part, part, share_send.at[where, i], share_recv.at[where, i], partner)

    def rides(i, up):
        return (side == (1 if up else 0)) if pieces[i][3] else (side >= 0)

    def text_step(s):
        for up in (True, False):
            where = place - s if up else place + s
            inside = (where >= 0) if up else (where < depth)
            on = has_up if up else has_down
            for i in range(len(pieces)):
                @pl.when(inside & rides(i, up))
                def _():
                    chain_copy(where, i, up).wait_recv()

                    @pl.when(on)
                    def _():
                        chain_copy(where, i, up).start()

                    if pieces[i][3]:
                        across_copy(where, i).start()
                    share_copy(where, i, core).start()

    def across_step(s):
        for up in (True, False):
            where = place - s if up else place + s
            inside = (where >= 0) if up else (where < depth)

            @pl.when(inside & jnp.logical_not(rides(1, up)))
            def _():
                for i in late:
                    across_copy(where, i).wait_recv()
                    share_copy(where, i, core).start()

    def text_sends_done(s):
        for up in (True, False):
            where = place - s if up else place + s
            inside = (where >= 0) if up else (where < depth)
            on = has_up if up else has_down
            for i in range(len(pieces)):
                @pl.when(inside)
                def _():
                    @pl.when(on & rides(i, up))
                    def _():
                        chain_copy(where, i, up).wait_send()

                    if pieces[i][3]:
                        @pl.when(rides(i, up))
                        def _():
                            across_copy(where, i).wait_send()

                    share_copy(where, i, core).wait_send()

    def shared(s, arrays):
        for up in (True, False):
            where = place - s if up else place + s
            inside = (where >= 0) if up else (where < depth)

            @pl.when(inside)
            def _():
                for i in arrays:
                    share_copy(where, i, 1 - core).wait_recv()

    def all_shared(arrays):
        for i in arrays:
            share_copy(place, i, 1 - core).wait_recv()
        lax.fori_loop(1, depth, lambda s, c: (shared(s, arrays), c)[1], 0)

    if relay_text:
        for i in range(2):
            half_copy(i, side).start()
    for g in range(min(AHEAD, GROUPS)):
        for i in range(2):
            near_copy(g, i).start()
            part_copy(g, i).start()
    for copy in local_copies():
        copy.wait()
    if relay_text:
        for i in range(2):
            half_copy(i, 1 - side).wait_recv()
        for i in range(len(pieces)):
            for up in (True, False):
                @pl.when((has_up if up else has_down) & rides(i, up))
                def _():
                    chain_copy(place, i, up).start()
            share_copy(place, i, core).start()

    scale = math.log2(math.e) / math.sqrt(head_dim)
    diag_slot = jnp.where(has_diag, DIAG, OWN)
    far_slot = jnp.where(has_far, FAR, OWN)

    def self_head(h):
        span = pl.ds(pl.multiple_of(h * head_dim, head_dim), head_dim)
        slots = (OWN, PARTNER, NEAR, diag_slot, far_slot)
        query = q_ref[:, span]
        keys = jnp.concatenate([kbuf[slot, :, span] for slot in slots], axis=0)
        values = jnp.concatenate([vbuf[slot, :, span] for slot in slots], axis=0)
        scores = scores_of(query, keys)
        blocks = [scores[:, n * tokens : (n + 1) * tokens] for n in range(5)]
        blocks[3] = jnp.where(has_diag, blocks[3], -1e30)
        blocks[4] = jnp.where(has_far, blocks[4], -1e30)
        rounded, total = softmax_parts(blocks, scale)
        summed = jnp.dot(rounded, values, preferred_element_type=jnp.float32)
        table = gate_ref[:, span].astype(jnp.float32)
        chosen = lax.broadcasted_iota(jnp.int32, table.shape, 0) == step_ref[0]
        gate = jnp.sum(jnp.where(chosen, table, 0.0), axis=0, keepdims=True)
        self_acc[:, span] = gate * (summed * (1.0 / total))

    def cross_scores(h):
        span = pl.ds(pl.multiple_of(h * head_dim, head_dim), head_dim)
        scores = scores_of(cq_ref[:, span], tkbuf[:, span])
        blocks = [scores[:, n * 128 : (n + 1) * 128] for n in range(scores.shape[1] // 128)]
        rounded, total = softmax_parts(blocks, scale)
        weight_ref[h] = rounded
        cross_acc[:, span] = jnp.broadcast_to(1.0 / total, (tokens, head_dim))

    def cross_values(h):
        span = pl.ds(pl.multiple_of(h * head_dim, head_dim), head_dim)
        summed = jnp.dot(weight_ref[h], tvbuf[:, span], preferred_element_type=jnp.float32)
        out_ref[:, span] = (self_acc[:, span] + summed * cross_acc[:, span]).astype(out_ref.dtype)

    def forward(g):
        for i in range(2):
            near_copy(g, i).wait_recv()

            @pl.when(has_ahead)
            def _():
                relay_copy(g, i).start()

            @pl.when(gives_near)
            def _():
                diag_copy(g, i, NEAR).start()

    def compute(g):
        for i in range(2):
            @pl.when(has_far)
            def _():
                far_copy(g, i).wait_recv()

                @pl.when(jnp.logical_not(gives_near))
                def _():
                    diag_copy(g, i, FAR).start()

        for i in range(2):
            part_copy(g, i).wait_recv()

            @pl.when(has_diag)
            def _():
                diag_copy(g, i, NEAR).wait_recv()

        for n in range(heads):
            self_head(g * heads + n)

    def round_of(r, carry):
        @pl.when(r < GROUPS)
        def _():
            forward(r)

        @pl.when(r + AHEAD < GROUPS)
        def _():
            for i in range(2):
                near_copy(r + AHEAD, i).start()
                part_copy(r + AHEAD, i).start()

        if relay_text:
            def one(s, c):
                @pl.when(r == jnp.minimum(s * TEXT_GAP - 1, GROUPS - 1))
                def _():
                    text_step(s)

                return c

            lax.fori_loop(1, depth, one, 0)

        @pl.when(r >= LAG)
        def _():
            compute(r - LAG)

        @pl.when(r >= SCORE_ROUND)
        def _():
            if relay_text:
                @pl.when(r == SCORE_ROUND)
                def _():
                    all_shared((0,))

            def four(n, c):
                for j in range(UNROLL):
                    cross_scores((r - SCORE_ROUND) * score_heads + UNROLL * n + j)
                return c

            lax.fori_loop(0, score_heads // UNROLL, four, 0)

        return carry

    score_heads = EARLY_HEADS // (GROUPS + LAG - SCORE_ROUND)
    lax.fori_loop(0, GROUPS + LAG, round_of, 0)

    if relay_text:
        lax.fori_loop(1, depth, lambda s, c: (across_step(s), c)[1], 0)
        all_shared(late)

    def late_scores(n, carry):
        for j in range(4):
            cross_scores(EARLY_HEADS + 4 * n + j)
        return carry

    lax.fori_loop(0, (HEADS - EARLY_HEADS) // 4, late_scores, 0)

    def cross_four(n, carry):
        for j in range(8):
            cross_values(8 * n + j)
        return carry

    lax.fori_loop(0, HEADS // 8, cross_four, 0)
    if relay_text:
        lax.fori_loop(1, depth, lambda s, c: (text_sends_done(s), c)[1], 0)

    def finish(g, carry):
        for i in range(2):
            near_copy(g, i).wait_send()
            part_copy(g, i).wait_send()

            @pl.when(has_ahead)
            def _():
                relay_copy(g, i).wait_send()

            @pl.when(gives_near | has_far)
            def _():
                diag_copy(g, i, NEAR).wait_send()

        return carry

    lax.fori_loop(0, GROUPS, finish, 0)
    if relay_text:
        for i in range(2):
            half_copy(i, side).wait_send()
        for i in range(len(pieces)):
            for up in (True, False):
                @pl.when((has_up if up else has_down) & rides(i, up))
                def _():
                    chain_copy(place, i, up).wait_send()
            share_copy(place, i, core).wait_send()


def shards(self_query, self_key, self_value, cross_query, text_key, text_value, timestep, gate_table):
    tiles = lax.axis_size("tile")
    depth = tiles // 4
    tokens, width = self_query.shape
    text_total = text_key.shape[0] * tiles
    relay_text = text_key.shape[0] % 16 == 0
    if not relay_text:
        text_key = lax.all_gather(text_key, "tile", axis=0, tiled=True)
        text_value = lax.all_gather(text_value, "tile", axis=0, tiled=True)
    anywhere = pl.BlockSpec(memory_space=pl.ANY)
    vmem = pl.BlockSpec(memory_space=pltpu.VMEM)
    smem = pl.BlockSpec(memory_space=pltpu.SMEM)
    dma = pltpu.SemaphoreType.DMA
    bf16, f32 = jnp.bfloat16, jnp.float32
    return pl.pallas_call(
        functools.partial(kernel, tiles, relay_text),
        out_shape=jax.ShapeDtypeStruct((tokens, width), bf16),
        in_specs=[smem] + [anywhere] * 7,
        out_specs=vmem,
        scratch_shapes=[
            pltpu.VMEM((tokens, width), bf16),
            pltpu.VMEM((tokens, width), bf16),
            pltpu.VMEM(gate_table.shape, bf16),
            pltpu.VMEM((5, tokens, width), bf16),
            pltpu.VMEM((5, tokens, width), bf16),
            pltpu.VMEM((text_total, width), bf16),
            pltpu.VMEM((text_total, width), bf16),
            pltpu.VMEM((tokens, width), f32),
            pltpu.VMEM((tokens, width), f32),
            pltpu.VMEM((HEADS, tokens, text_total), bf16),
            dma((5,)),
            dma((2,)),
        ]
        + [dma((GROUPS, 2))] * 8
        + [dma((2,)), dma((2,)), dma((depth, 3, 2))] + [dma((depth, 3))] * 4,
        compiler_params=pltpu.CompilerParams(
            collective_id=0, has_side_effects=True, vmem_limit_bytes=60 * 1024 * 1024
        ),
    )(timestep, self_query, self_key, self_value, cross_query, text_key, text_value, gate_table)


def solution(mesh):
    rows = P(("groups", "tile"), None)
    return jax.shard_map(
        shards, mesh=mesh, in_specs=(rows,) * 6 + (P(), P()), out_specs=rows, check_vma=False
    )
```

profile of v0, /device:TPU:6, one launch (start us, length us, event | category | flops | bytes accessed | tf_op | source)
XLA Modules:
  0.0 84.5 jit_solution(15539908448983538881)
XLA Ops:
  0.7 81.5 %shard_map.82 = bf16[128,4096]{1,0:T(8,128)(2,1)} custom-call(s32[1]{0:T(128)S(6)} %copy.10.step_ref, bf16[128,4096]{1,0:T(8,128)(2,1)} %q_hbm.1, bf16[128,4096]{1,0:T(8,128)(2,1)} %k_hbm.1, bf16[128,4096]{1,0:T(8,128)(2,1)} %v_hbm.1, bf16[128,4096]{1,0:T(8,128)(2,1)} %cq_hbm.1, bf16[16,4096]{1,0:T(8,128)(2,1)} %tk_hbm.1, bf16[16,4096]{1,0:T(8,128)(2,1)} %tv_hbm.1, ...), custom_call_target="tpu_custom_call" | custom-call | tf_op jit(solution)/shard_map/pallas_call | solution.py:441
  82.2 2.3 %copy.11 = bf16[128,4096]{1,0:T(8,128)(2,1)} copy(bf16[128,4096]{1,0:T(8,128)(2,1)} %shard_map.82) | data formatting | bytes 2097152
where the time goes:
time: 84.6 us; the launch traced here: 84.5 us
  Pallas kernels  81.5 us (96%)
  local copies, waits for them, and re-layouts  2.29 us (3%)
    pallas_call x1, Pallas kernels, shards(): pl.pallas_call(functools.partial(kernel, tiles, relay_text), out_shape=ja...  81.5 us
    unnamed x1, local copies, waits for them, and re-layouts  2.29 us

commit v1 on v0

v1 whole, which is shorter than its diff:
```python
import functools
import math

import jax
import jax.numpy as jnp
from jax import lax
from jax.experimental import pallas as pl
from jax.experimental.pallas import tpu as pltpu
from jax.sharding import PartitionSpec as P

HEADS = 32
RADIUS = 2
PLANE = 4
WINDOW = PLANE + 2 * RADIUS
CHUNKS = 8
LAG = 2
PARTS = 2
FIRST_TEXT_ROUND = 2
SECOND_TEXT_ROUND = 8
UNROLL = 4
MESH = pl.DeviceIdType.MESH


def softmax_parts(scores, scale):
    top = scores[0]
    for block in scores[1:]:
        top = jnp.maximum(top, block)
    top = jnp.max(top, axis=1, keepdims=True)
    weights = [jnp.exp2((block - top) * scale) for block in scores]
    total = weights[0]
    for block in weights[1:]:
        total = total + block
    total = jnp.sum(total, axis=1, keepdims=True)
    rounded = jnp.concatenate([block.astype(jnp.bfloat16) for block in weights], axis=1)
    return rounded, total


def scores_of(query, keys):
    return lax.dot_general(query, keys, (((1,), (1,)), ((), ())), preferred_element_type=jnp.float32)


def kernel(
    tiles, relay_text, step_ref, q_hbm, k_hbm, v_hbm, cq_hbm, tk_hbm, tv_hbm, gate_hbm, out_ref,
    qbuf, kvbuf, tbuf, cq_ref, gate_ref, gate_row, o32, o16, precv, orecv, inv_ref, weight_ref,
    local_sem, a2a_send, a2a_recv, halo_send, halo_recv, o_send, o_recv,
    half_send, half_recv, chain_send, chain_recv, share_send, share_recv,
):
    tokens, width = cq_ref.shape
    head_dim = width // HEADS
    quarter = width // PLANE
    columns = quarter // CHUNKS
    heads = columns // head_dim
    depth = tiles // PLANE
    text_rows = tk_hbm.shape[0]
    pieces = 2 * PARTS
    piece_columns = width // PARTS
    reach = RADIUS * tokens

    t = lax.axis_index("tile")
    core = lax.rem(t, 2)
    side = lax.rem(t // 2, 2)
    place = t // PLANE
    me = t - place * PLANE
    has_up = place < depth - 1
    has_down = place > 0

    def other(m):
        step = 0
        if m % 2:
            step = step + 1 - 2 * core
        if m // 2:
            step = step + 2 - 4 * side
        return step

    def remote(src, dst, send, recv, device):
        return pltpu.make_async_remote_copy(
            src_ref=src, dst_ref=dst, send_sem=send, recv_sem=recv, device_id={"tile": device}, device_id_type=MESH
        )

    def cols(start, size):
        return pl.ds(pl.multiple_of(start, size), size)

    def rows(start, size):
        return pl.ds(pl.multiple_of(start, size), size)

    sources = (k_hbm, v_hbm, q_hbm)
    texts = (tk_hbm, tv_hbm)

    def slot_rows(i, device):
        return rows((device + (RADIUS if i < 2 else 0)) * tokens, tokens)

    def landing(i):
        return kvbuf.at[i] if i < 2 else qbuf

    def local_copies():
        copies = [
            pltpu.make_async_copy(cq_hbm, cq_ref, local_sem.at[0]),
            pltpu.make_async_copy(gate_hbm.at[:, cols(me * quarter, quarter)], gate_ref, local_sem.at[1]),
        ]
        for i in range(3):
            copies.append(
                pltpu.make_async_copy(
                    sources[i].at[:, cols(me * quarter, quarter)], landing(i).at[slot_rows(i, me), :], local_sem.at[2 + i]
                )
            )
        for i in range(2):
            where = text_half(place, side) if relay_text else slice(None)
            copies.append(pltpu.make_async_copy(texts[i], tbuf.at[i, where, :], local_sem.at[5 + i]))
        return copies

    def text_half(where, half):
        return rows(((where * 2 + core) * 2 + half) * text_rows, text_rows)

    def text_pair(where, which):
        return rows((where * 2 + which) * 2 * text_rows, 2 * text_rows)

    def a2a_copy(c, m, i):
        device = me + other(m)
        return remote(
            sources[i].at[:, cols(device * quarter + c * columns, columns)],
            landing(i).at[slot_rows(i, me), cols(c * columns, columns)],
            a2a_send.at[c, m - 1, i], a2a_recv.at[c, m - 1, i], t + other(m),
        )

    def a2a_arrival(c, m, i):
        device = me + other(m)
        part = landing(i).at[slot_rows(i, device), cols(c * columns, columns)]
        return remote(part, part, a2a_send.at[c, m - 1, i], a2a_recv.at[c, m - 1, i], t + other(m))

    def halo_copy(c, up, i):
        start, end = (PLANE * tokens, 0) if up else (reach, WINDOW * tokens - reach)
        span = cols(c * columns, columns)
        return remote(
            kvbuf.at[i, pl.ds(start, reach), span], kvbuf.at[i, pl.ds(end, reach), span],
            halo_send.at[c, int(up), i], halo_recv.at[c, int(up), i], t + (PLANE if up else -PLANE),
        )

    def o_copy(c, m):
        device = me + other(m)
        span = cols(c * columns, columns)
        if m == 1:
            source, target = o32.at[rows(device * tokens, tokens), span], precv.at[:, span]
        else:
            source, target = o16.at[rows(device * tokens, tokens), span], orecv.at[m - 2, :, span]
        return remote(source, target, o_send.at[c, m - 1], o_recv.at[c, m - 1], t + other(m))

    def part_columns(n):
        return cols((n % PARTS) * piece_columns, piece_columns)

    def half_copy(n, half):
        i = n // PARTS
        return remote(
            texts[i].at[:, part_columns(n)], tbuf.at[i, text_half(place, half), part_columns(n)],
            half_send.at[n], half_recv.at[n], t + other(2),
        )

    def chain_copy(where, half, n, up):
        part = tbuf.at[n // PARTS, text_half(where, half), part_columns(n)]
        return remote(
            part, part, chain_send.at[where, half, n, int(up)], chain_recv.at[where, half, n],
            t + (PLANE if up else -PLANE),
        )

    def share_copy(where, which, n):
        part = tbuf.at[n // PARTS, text_pair(where, which), part_columns(n)]
        return remote(part, part, share_send.at[where, n], share_recv.at[where, n], t + other(1))

    def ways(s):
        return ((True, place - s, place - s >= 0, has_up), (False, place + s, place + s < depth, has_down))

    def text_step(s, n):
        for up, where, inside, on in ways(s):
            @pl.when(inside)
            def _():
                for half in range(2):
                    chain_copy(where, half, n, up).wait_recv()

                    @pl.when(on)
                    def _():
                        chain_copy(where, half, n, up).start()

                share_copy(where, core, n).start()

    def text_steps(s, first, last):
        lax.fori_loop(first, last, lambda n, c: (text_step(s, n), c)[1], 0)

    def first_chain(half, n):
        for up, on in ((True, has_up), (False, has_down)):
            @pl.when(on)
            def _():
                chain_copy(place, half, n, up).start()

    def shared(n):
        def one(where, c):
            share_copy(where, 1 - core, n).wait_recv()
            return c

        lax.fori_loop(0, depth, one, 0)

    for copy in local_copies():
        copy.start()

    barrier = pltpu.get_barrier_semaphore()

    def greet(device):
        pl.semaphore_signal(barrier, inc=1, device_id={"tile": device}, device_id_type=MESH)

    for m in range(1, PLANE):
        greet(t + other(m))

    @pl.when(has_up)
    def _():
        greet(t + PLANE)

    @pl.when(has_down)
    def _():
        greet(t - PLANE)

    pl.semaphore_wait(barrier, PLANE - 1 + has_up.astype(jnp.int32) + has_down.astype(jnp.int32))

    def send_chunk(c):
        for i in range(3):
            for m in (2, 3, 1):
                a2a_copy(c, m, i).start()

    send_chunk(0)
    if relay_text:
        for n in range(PARTS):
            half_copy(n, side).start()
    send_chunk(1)
    if relay_text:
        for n in range(PARTS, pieces):
            half_copy(n, side).start()

    for copy in local_copies():
        copy.wait()
    if relay_text:
        for n in range(pieces):
            for up, on in ((True, has_up), (False, has_down)):
                @pl.when(on)
                def _():
                    chain_copy(place, side, n, up).start()

    lax.fori_loop(2, CHUNKS, lambda c, z: (send_chunk(c), z)[1], 0)

    table = gate_ref[...].astype(jnp.float32)
    chosen = lax.broadcasted_iota(jnp.int32, table.shape, 0) == step_ref[0]
    gate_row[...] = jnp.sum(jnp.where(chosen, table, 0.0), axis=0, keepdims=True)

    @pl.when(jnp.logical_not(has_down))
    def _():
        kvbuf[:, 0:reach, :] = jnp.zeros((2, reach, quarter), jnp.bfloat16)

    @pl.when(jnp.logical_not(has_up))
    def _():
        kvbuf[:, WINDOW * tokens - reach :, :] = jnp.zeros((2, reach, quarter), jnp.bfloat16)

    scale = math.log2(math.e) / math.sqrt(head_dim)

    def self_head(h, i):
        span = cols(h * head_dim, head_dim)
        query = qbuf[i * tokens : (i + 1) * tokens, span]
        window = slice(i * tokens, (i + 2 * RADIUS + 1) * tokens)
        scores = scores_of(query, kvbuf[0, window, span])
        blocks = []
        for n in range(2 * RADIUS + 1):
            block = scores[:, n * tokens : (n + 1) * tokens]
            if i + n < RADIUS:
                block = jnp.where(has_down, block, -1e30)
            if i + n >= WINDOW - RADIUS:
                block = jnp.where(has_up, block, -1e30)
            blocks.append(block)
        rounded, total = softmax_parts(blocks, scale)
        summed = jnp.dot(rounded, kvbuf[1, window, span], preferred_element_type=jnp.float32)
        result = gate_row[:, span] * (summed * (1.0 / total))
        o32[i * tokens : (i + 1) * tokens, span] = result
        o16[i * tokens : (i + 1) * tokens, span] = result.astype(jnp.bfloat16)

    def cross_scores(h):
        span = cols(h * head_dim, head_dim)
        scores = scores_of(cq_ref[:, span], tbuf[0, :, span])
        blocks = [scores[:, n * 128 : (n + 1) * 128] for n in range(scores.shape[1] // 128)]
        rounded, total = softmax_parts(blocks, scale)
        weight_ref[h] = rounded
        inv_ref[:, span] = jnp.broadcast_to(1.0 / total, (tokens, head_dim))

    def combine(h, m, k):
        span = cols(h * head_dim, head_dim)
        own = cols(k * head_dim, head_dim)
        if m == 0:
            part = o32[rows(me * tokens, tokens), own]
        elif m == 1:
            part = precv[:, own]
        else:
            part = orecv[m - 2, :, own].astype(jnp.float32)
        summed = jnp.dot(weight_ref[h], tbuf[1, :, span], preferred_element_type=jnp.float32)
        out_ref[:, span] = (part + summed * inv_ref[:, span]).astype(out_ref.dtype)

    def forward(c):
        for i in range(2):
            for m in (1, 2, 3):
                a2a_arrival(c, m, i).wait_recv()
            for up, on in ((True, has_up), (False, has_down)):
                @pl.when(on)
                def _():
                    halo_copy(c, up, i).start()

    def compute(c):
        for m in (1, 2, 3):
            a2a_arrival(c, m, 2).wait_recv()
        for i in range(2):
            for up, on in ((True, has_down), (False, has_up)):
                @pl.when(on)
                def _():
                    halo_copy(c, up, i).wait_recv()
        for k in range(heads):
            for i in range(PLANE):
                self_head(c * heads + k, i)

    def give(c):
        for m in (2, 3, 1):
            o_copy(c, m).start()

    def round_of(r, carry):
        @pl.when(r < CHUNKS)
        def _():
            forward(r)

        if relay_text:
            for n in range(2):
                @pl.when(r == n)
                def _():
                    for j in range(n * PARTS, (n + 1) * PARTS):
                        half_copy(j, 1 - side).wait_recv()
                        first_chain(1 - side, j)
                        share_copy(place, core, j).start()

            if depth > 1:
                @pl.when(r == FIRST_TEXT_ROUND)
                def _():
                    text_steps(1, 0, PARTS)

                @pl.when(r == FIRST_TEXT_ROUND + 1)
                def _():
                    text_steps(1, PARTS, pieces)

            if depth > 2:
                @pl.when(r == SECOND_TEXT_ROUND)
                def _():
                    text_steps(2, 0, pieces)

        @pl.when(r >= LAG)
        def _():
            compute(r - LAG)

        @pl.when(r > LAG)
        def _():
            give(r - LAG - 1)

        return carry

    lax.fori_loop(0, CHUNKS + LAG, round_of, 0)
    give(CHUNKS - 1)

    if relay_text:
        lax.fori_loop(3, depth, lambda s, c: (text_steps(s, 0, PARTS), c)[1], 0)
        for n in range(PARTS):
            shared(n)

    def scores_four(n, carry):
        for j in range(UNROLL):
            cross_scores(UNROLL * n + j)
        return carry

    lax.fori_loop(0, HEADS // UNROLL, scores_four, 0)

    if relay_text:
        lax.fori_loop(3, depth, lambda s, c: (text_steps(s, PARTS, pieces), c)[1], 0)

    def o_arrivals(c, carry):
        for m in (1, 2, 3):
            o_copy(c, m).wait_recv()
        return carry

    lax.fori_loop(0, CHUNKS, o_arrivals, 0)
    if relay_text:
        for n in range(PARTS, pieces):
            shared(n)

    per = HEADS // PLANE
    for m in range(PLANE):
        def combine_four(n, carry):
            for j in range(UNROLL):
                k = UNROLL * n + j
                combine((me + other(m)) * per + k, m, k)
            return carry

        lax.fori_loop(0, per // UNROLL, combine_four, 0)

    def finish(c, carry):
        for m in (1, 2, 3):
            for i in range(3):
                a2a_copy(c, m, i).wait_send()
            o_copy(c, m).wait_send()
        for i in range(2):
            for up, on in ((True, has_up), (False, has_down)):
                @pl.when(on)
                def _():
                    halo_copy(c, up, i).wait_send()
        return carry

    lax.fori_loop(0, CHUNKS, finish, 0)

    if relay_text:
        for n in range(pieces):
            half_copy(n, side).wait_send()

        def finish_text(s, carry):
            def one(n, c):
                for up, where, inside, on in ways(s):
                    @pl.when(inside & on)
                    def _():
                        for half in range(2):
                            chain_copy(where, half, n, up).wait_send()

                return c

            lax.fori_loop(0, pieces, one, 0)
            return carry

        lax.fori_loop(0, depth, finish_text, 0)

        def finish_share(where, carry):
            lax.fori_loop(0, pieces, lambda n, c: (share_copy(where, core, n).wait_send(), c)[1], 0)
            return carry

        lax.fori_loop(0, depth, finish_share, 0)


def shards(self_query, self_key, self_value, cross_query, text_key, text_value, timestep, gate_table):
    tiles = lax.axis_size("tile")
    depth = tiles // PLANE
    tokens, width = self_query.shape
    quarter = width // PLANE
    text_total = text_key.shape[0] * tiles
    relay_text = text_key.shape[0] % 16 == 0
    if not relay_text:
        text_key = lax.all_gather(text_key, "tile", axis=0, tiled=True)
        text_value = lax.all_gather(text_value, "tile", axis=0, tiled=True)
    anywhere = pl.BlockSpec(memory_space=pl.ANY)
    vmem = pl.BlockSpec(memory_space=pltpu.VMEM)
    smem = pl.BlockSpec(memory_space=pltpu.SMEM)
    dma = pltpu.SemaphoreType.DMA
    bf16, f32 = jnp.bfloat16, jnp.float32
    held = depth if relay_text else 1
    pieces = 2 * PARTS
    return pl.pallas_call(
        functools.partial(kernel, tiles, relay_text),
        out_shape=jax.ShapeDtypeStruct((tokens, width), bf16),
        in_specs=[smem] + [anywhere] * 7,
        out_specs=vmem,
        scratch_shapes=[
            pltpu.VMEM((PLANE * tokens, quarter), bf16),
            pltpu.VMEM((2, WINDOW * tokens, quarter), bf16),
            pltpu.VMEM((2, text_total, width), bf16),
            pltpu.VMEM((tokens, width), bf16),
            pltpu.VMEM((gate_table.shape[0], quarter), bf16),
            pltpu.VMEM((1, quarter), f32),
            pltpu.VMEM((PLANE * tokens, quarter), f32),
            pltpu.VMEM((PLANE * tokens, quarter), bf16),
            pltpu.VMEM((tokens, quarter), f32),
            pltpu.VMEM((2, tokens, quarter), bf16),
            pltpu.VMEM((tokens, width), f32),
            pltpu.VMEM((HEADS, tokens, text_total), bf16),
            dma((7,)),
            dma((CHUNKS, PLANE - 1, 3)),
            dma((CHUNKS, PLANE - 1, 3)),
            dma((CHUNKS, 2, 2)),
            dma((CHUNKS, 2, 2)),
            dma((CHUNKS, PLANE - 1)),
            dma((CHUNKS, PLANE - 1)),
            dma((pieces,)),
            dma((pieces,)),
            dma((held, 2, pieces, 2)),
            dma((held, 2, pieces)),
            dma((held, pieces)),
            dma((held, pieces)),
        ],
        compiler_params=pltpu.CompilerParams(
            collective_id=0, has_side_effects=True, vmem_limit_bytes=60 * 1024 * 1024
        ),
    )(timestep, self_query, self_key, self_value, cross_query, text_key, text_value, gate_table)


def solution(mesh):
    rows = P(("groups", "tile"), None)
    return jax.shard_map(
        shards, mesh=mesh, in_specs=(rows,) * 6 + (P(), P()), out_specs=rows, check_vma=False
    )
```

time: 84.6 us -> 74.8 us (0.88)
  the two profiles are of different devices: /device:TPU:6 before, /device:TPU:0 now
where the time goes in v1:
time: 74.8 us; the launch traced here: 74.7 us
  Pallas kernels  71.7 us (96%)
  local copies, waits for them, and re-layouts  2.29 us (3%)
    pallas_call x1, Pallas kernels, shards(): pl.pallas_call(functools.partial(kernel, tiles, relay_text), out_shape=ja...  71.7 us
    unnamed x1, local copies, waits for them, and re-layouts  2.29 us

profile of v1, /device:TPU:0, one launch (start us, length us, event | category | flops | bytes accessed | tf_op | source)
XLA Modules:
  0.0 74.7 jit_solution(8811674247261572146)
XLA Ops:
  0.7 71.7 %shard_map.82 = bf16[128,4096]{1,0:T(8,128)(2,1)} custom-call(s32[1]{0:T(128)S(6)} %copy.10.step_ref, bf16[128,4096]{1,0:T(8,128)(2,1)} %q_hbm.1, bf16[128,4096]{1,0:T(8,128)(2,1)} %k_hbm.1, bf16[128,4096]{1,0:T(8,128)(2,1)} %v_hbm.1, bf16[128,4096]{1,0:T(8,128)(2,1)} %cq_hbm.1, bf16[16,4096]{1,0:T(8,128)(2,1)} %tk_hbm.1, bf16[16,4096]{1,0:T(8,128)(2,1)} %tv_hbm.1, ...), custom_call_target="tpu_custom_call" | custom-call | tf_op jit(solution)/shard_map/pallas_call | solution.py:457
  72.4 2.3 %copy.11 = bf16[128,4096]{1,0:T(8,128)(2,1)} copy(bf16[128,4096]{1,0:T(8,128)(2,1)} %shard_map.82) | data formatting | bytes 2097152

commit v2 on v1

--- a/solution.py
+++ b/solution.py
@@ -12,12 +12,14 @@
 RADIUS = 2
 PLANE = 4
 WINDOW = PLANE + 2 * RADIUS
+PAIRS = 4
 CHUNKS = 8
-LAG = 2
 PARTS = 2
-FIRST_TEXT_ROUND = 2
-SECOND_TEXT_ROUND = 8
+HALF_ROUNDS = (0, 1)
+FIRST_ROUNDS = (1, 1, 2, 2)
+SECOND_ROUNDS = (0, 0, 2, 2)
 UNROLL = 4
+CROSSING = ((2,), (3,))
 MESH = pl.DeviceIdType.MESH
 
 
@@ -42,13 +44,14 @@
 def kernel(
     tiles, relay_text, step_ref, q_hbm, k_hbm, v_hbm, cq_hbm, tk_hbm, tv_hbm, gate_hbm, out_ref,
     qbuf, kvbuf, tbuf, cq_ref, gate_ref, gate_row, o32, o16, precv, orecv, inv_ref, weight_ref,
-    local_sem, a2a_send, a2a_recv, halo_send, halo_recv, o_send, o_recv,
-    half_send, half_recv, chain_send, chain_recv, share_send, share_recv,
+    local_sem, pair_send, pair_recv, q_send, q_recv, halo_send, halo_recv, o_send, o_recv,
+    half_send, half_recv, chain_send, chain_recv, share_send, share_recv, cross_send, cross_recv,
 ):
     tokens, width = cq_ref.shape
     head_dim = width // HEADS
     quarter = width // PLANE
     columns = quarter // CHUNKS
+    paired = quarter // PAIRS
     heads = columns // head_dim
     depth = tiles // PLANE
     text_rows = tk_hbm.shape[0]
@@ -114,22 +117,33 @@
     def text_pair(where, which):
         return rows((where * 2 + which) * 2 * text_rows, 2 * text_rows)
 
-    def a2a_copy(c, m, i):
+    def pair_copy(c, m, i):
         device = me + other(m)
         return remote(
-            sources[i].at[:, cols(device * quarter + c * columns, columns)],
-            landing(i).at[slot_rows(i, me), cols(c * columns, columns)],
-            a2a_send.at[c, m - 1, i], a2a_recv.at[c, m - 1, i], t + other(m),
+            sources[i].at[:, cols(device * quarter + c * paired, paired)],
+            landing(i).at[slot_rows(i, me), cols(c * paired, paired)],
+            pair_send.at[c, m - 1, i], pair_recv.at[c, m - 1, i], t + other(m),
         )
 
-    def a2a_arrival(c, m, i):
+    def pair_arrival(c, m, i):
+        part = landing(i).at[slot_rows(i, me + other(m)), cols(c * paired, paired)]
+        return remote(part, part, pair_send.at[c, m - 1, i], pair_recv.at[c, m - 1, i], t + other(m))
+
+    def q_copy(c, m):
         device = me + other(m)
-        part = landing(i).at[slot_rows(i, device), cols(c * columns, columns)]
-        return remote(part, part, a2a_send.at[c, m - 1, i], a2a_recv.at[c, m - 1, i], t + other(m))
+        return remote(
+            q_hbm.at[:, cols(device * quarter + c * columns, columns)],
+            qbuf.at[slot_rows(2, me), cols(c * columns, columns)],
+            q_send.at[c, m - 1], q_recv.at[c, m - 1], t + other(m),
+        )
+
+    def q_arrival(c, m):
+        part = qbuf.at[slot_rows(2, me + other(m)), cols(c * columns, columns)]
+        return remote(part, part, q_send.at[c, m - 1], q_recv.at[c, m - 1], t + other(m))
 
     def halo_copy(c, up, i):
         start, end = (PLANE * tokens, 0) if up else (reach, WINDOW * tokens - reach)
-        span = cols(c * columns, columns)
+        span = cols(c * paired, paired)
         return remote(
             kvbuf.at[i, pl.ds(start, reach), span], kvbuf.at[i, pl.ds(end, reach), span],
             halo_send.at[c, int(up), i], halo_recv.at[c, int(up), i], t + (PLANE if up else -PLANE),
@@ -165,6 +179,16 @@
         part = tbuf.at[n // PARTS, text_pair(where, which), part_columns(n)]
         return remote(part, part, share_send.at[where, n], share_recv.at[where, n], t + other(1))
 
+    def cross_copy(where, half, n):
+        part = tbuf.at[n // PARTS, text_half(where, half), part_columns(n)]
+        return remote(part, part, cross_send.at[half, n], cross_recv.at[half, n], t + other(2))
+
+    crossing = depth > 2
+
+    def crosses(n):
+        sides = [y for y in range(2) if n in CROSSING[y]] if crossing else []
+        return side == sides[0] if sides else None
+
     def ways(s):
         return ((True, place - s, place - s >= 0, has_up), (False, place + s, place + s < depth, has_down))
 
@@ -184,9 +208,49 @@
     def text_steps(s, first, last):
         lax.fori_loop(first, last, lambda n, c: (text_step(s, n), c)[1], 0)
 
+    def first_step(n):
+        late = crosses(n)
+        if late is None:
+            text_step(1, n)
+            return
+        for up, where, inside, on in ways(1):
+            end = place == (depth - 1 if up else 0)
+
+            @pl.when(inside & jnp.logical_not(end & late))
+            def _():
+                for half in range(2):
+                    chain_copy(where, half, n, up).wait_recv()
+
+                    @pl.when(on)
+                    def _():
+                        chain_copy(where, half, n, up).start()
+
+                    @pl.when(end)
+                    def _():
+                        cross_copy(where, half, n).start()
+
+                share_copy(where, core, n).start()
+
+    def crossed():
+        for n in range(pieces):
+            late = crosses(n)
+            if late is not None:
+                for up, where, inside, on in ways(1):
+                    @pl.when((place == (depth - 1 if up else 0)) & late)
+                    def _():
+                        for half in range(2):
+                            cross_copy(where, half, n).wait_recv()
+                        share_copy(where, core, n).start()
+
+    def first_on(n, up, on):
+        late = crosses(n)
+        if late is None:
+            return on
+        return on & jnp.logical_not(late & (place == (depth - 2 if up else 1)))
+
     def first_chain(half, n):
         for up, on in ((True, has_up), (False, has_down)):
-            @pl.when(on)
+            @pl.when(first_on(n, up, on))
             def _():
                 chain_copy(place, half, n, up).start()
 
@@ -218,30 +282,33 @@
 
     pl.semaphore_wait(barrier, PLANE - 1 + has_up.astype(jnp.int32) + has_down.astype(jnp.int32))
 
-    def send_chunk(c):
-        for i in range(3):
+    def send_pair(c):
+        for i in range(2):
             for m in (2, 3, 1):
-                a2a_copy(c, m, i).start()
-
-    send_chunk(0)
+                pair_copy(c, m, i).start()
+
+    def send_query(c, carry):
+        for m in (2, 3, 1):
+            q_copy(c, m).start()
+        return carry
+
+    copies = local_copies()
+    send_pair(0)
     if relay_text:
-        for n in range(PARTS):
-            half_copy(n, side).start()
-    send_chunk(1)
-    if relay_text:
-        for n in range(PARTS, pieces):
-            half_copy(n, side).start()
-
-    for copy in local_copies():
+        for copy in copies[5:]:
+            copy.wait()
+        for n in range(pieces):
+            first_chain(side, n)
+    for c in range(1, PAIRS):
+        if relay_text:
+            for j in range(2):
+                if HALF_ROUNDS[j] == c - 1:
+                    for n in range(j * PARTS, (j + 1) * PARTS):
+                        half_copy(n, side).start()
+        send_pair(c)
+    lax.fori_loop(0, CHUNKS, send_query, 0)
+    for copy in copies if not relay_text else copies[:5]:
         copy.wait()
-    if relay_text:
-        for n in range(pieces):
-            for up, on in ((True, has_up), (False, has_down)):
-                @pl.when(on)
-                def _():
-                    chain_copy(place, side, n, up).start()
-
-    lax.fori_loop(2, CHUNKS, lambda c, z: (send_chunk(c), z)[1], 0)
 
     table = gate_ref[...].astype(jnp.float32)
     chosen = lax.broadcasted_iota(jnp.int32, table.shape, 0) == step_ref[0]
@@ -284,35 +351,47 @@
         weight_ref[h] = rounded
         inv_ref[:, span] = jnp.broadcast_to(1.0 / total, (tokens, head_dim))
 
-    def combine(h, m, k):
+    def cross_values(h):
         span = cols(h * head_dim, head_dim)
-        own = cols(k * head_dim, head_dim)
+        summed = jnp.dot(weight_ref[h], tbuf[1, :, span], preferred_element_type=jnp.float32)
+        inv_ref[:, span] = summed * inv_ref[:, span]
+
+    def combine(c, m):
+        span = cols((me + other(m)) * quarter + c * columns, columns)
+        own = cols(c * columns, columns)
         if m == 0:
             part = o32[rows(me * tokens, tokens), own]
         elif m == 1:
             part = precv[:, own]
         else:
             part = orecv[m - 2, :, own].astype(jnp.float32)
-        summed = jnp.dot(weight_ref[h], tbuf[1, :, span], preferred_element_type=jnp.float32)
-        out_ref[:, span] = (part + summed * inv_ref[:, span]).astype(out_ref.dtype)
+        out_ref[:, span] = (part + inv_ref[:, span]).astype(out_ref.dtype)
 
     def forward(c):
         for i in range(2):
             for m in (1, 2, 3):
-                a2a_arrival(c, m, i).wait_recv()
+                pair_arrival(c, m, i).wait_recv()
             for up, on in ((True, has_up), (False, has_down)):
                 @pl.when(on)
                 def _():
                     halo_copy(c, up, i).start()
 
-    def compute(c):
-        for m in (1, 2, 3):
-            a2a_arrival(c, m, 2).wait_recv()
+    def halos(c):
         for i in range(2):
             for up, on in ((True, has_down), (False, has_up)):
                 @pl.when(on)
                 def _():
                     halo_copy(c, up, i).wait_recv()
+
+    def compute(c):
+        each = CHUNKS // PAIRS
+        for m in (1, 2, 3):
+            q_arrival(c, m).wait_recv()
+
+        @pl.when(lax.rem(c, each) == 0)
+        def _():
+            halos(c // each)
+
         for k in range(heads):
             for i in range(PLANE):
                 self_head(c * heads + k, i)
@@ -321,45 +400,40 @@
         for m in (2, 3, 1):
             o_copy(c, m).start()
 
-    def round_of(r, carry):
-        @pl.when(r < CHUNKS)
+    def text_turns(r, row, step):
+        for turn in sorted(set(row)):
+            @pl.when(r == turn)
+            def _():
+                for n in range(pieces):
+                    if row[n] == turn:
+                        step(n)
+
+    def half_step(n):
+        half_copy(n, 1 - side).wait_recv()
+        first_chain(1 - side, n)
+        share_copy(place, core, n).start()
+
+    def forward_round(r, carry):
+        forward(r)
+        if relay_text:
+            text_turns(r, [HALF_ROUNDS[n // PARTS] for n in range(pieces)], half_step)
+            if depth > 1:
+                text_turns(r, FIRST_ROUNDS, first_step)
+        return carry
+
+    def compute_round(c, carry):
+        compute(c)
+
+        @pl.when(c > 0)
         def _():
-            forward(r)
-
-        if relay_text:
-            for n in range(2):
-                @pl.when(r == n)
-                def _():
-                    for j in range(n * PARTS, (n + 1) * PARTS):
-                        half_copy(j, 1 - side).wait_recv()
-                        first_chain(1 - side, j)
-                        share_copy(place, core, j).start()
-
-            if depth > 1:
-                @pl.when(r == FIRST_TEXT_ROUND)
-                def _():
-                    text_steps(1, 0, PARTS)
-
-                @pl.when(r == FIRST_TEXT_ROUND + 1)
-                def _():
-                    text_steps(1, PARTS, pieces)
-
-            if depth > 2:
-                @pl.when(r == SECOND_TEXT_ROUND)
-                def _():
-                    text_steps(2, 0, pieces)
-
-        @pl.when(r >= LAG)
-        def _():
-            compute(r - LAG)
-
-        @pl.when(r > LAG)
-        def _():
-            give(r - LAG - 1)
-
-        return carry
-
-    lax.fori_loop(0, CHUNKS + LAG, round_of, 0)
+            give(c - 1)
+
+        if relay_text and depth > 2:
+            text_turns(c, SECOND_ROUNDS, functools.partial(text_step, 2))
+        return carry
+
+    lax.fori_loop(0, PAIRS, forward_round, 0)
+    lax.fori_loop(0, CHUNKS, compute_round, 0)
     give(CHUNKS - 1)
 
     if relay_text:
@@ -375,34 +449,40 @@
     lax.fori_loop(0, HEADS // UNROLL, scores_four, 0)
 
     if relay_text:
+        crossed()
         lax.fori_loop(3, depth, lambda s, c: (text_steps(s, PARTS, pieces), c)[1], 0)
 
-    def o_arrivals(c, carry):
-        for m in (1, 2, 3):
-            o_copy(c, m).wait_recv()
-        return carry
-
-    lax.fori_loop(0, CHUNKS, o_arrivals, 0)
-    if relay_text:
-        for n in range(PARTS, pieces):
-            shared(n)
-
-    per = HEADS // PLANE
-    for m in range(PLANE):
-        def combine_four(n, carry):
-            for j in range(UNROLL):
-                k = UNROLL * n + j
-                combine((me + other(m)) * per + k, m, k)
-            return carry
-
-        lax.fori_loop(0, per // UNROLL, combine_four, 0)
+    per = HEADS // PARTS // UNROLL
+
+    def values_four(n, carry):
+        for j in range(UNROLL):
+            cross_values(UNROLL * n + j)
+        return carry
+
+    for n in range(PARTS):
+        if relay_text:
+            shared(PARTS + n)
+        lax.fori_loop(n * per, (n + 1) * per, values_four, 0)
+
+    def combine_chunk(c, carry):
+        for m in range(PLANE):
+            if m:
+                o_copy(c, m).wait_recv()
+            combine(c, m)
+        return carry
+
+    lax.fori_loop(0, CHUNKS, combine_chunk, 0)
 
     def finish(c, carry):
         for m in (1, 2, 3):
-            for i in range(3):
-                a2a_copy(c, m, i).wait_send()
+            q_copy(c, m).wait_send()
             o_copy(c, m).wait_send()
+        return carry
+
+    def finish_pair(c, carry):
         for i in range(2):
+            for m in (1, 2, 3):
+                pair_copy(c, m, i).wait_send()
             for up, on in ((True, has_up), (False, has_down)):
                 @pl.when(on)
                 def _():
@@ -410,10 +490,26 @@
         return carry
 
     lax.fori_loop(0, CHUNKS, finish, 0)
+    lax.fori_loop(0, PAIRS, finish_pair, 0)
 
     if relay_text:
         for n in range(pieces):
             half_copy(n, side).wait_send()
+
+        for n in range(pieces):
+            for up, on in ((True, has_up), (False, has_down)):
+                @pl.when(first_on(n, up, on))
+                def _():
+                    for half in range(2):
+                        chain_copy(place, half, n, up).wait_send()
+
+            late = crosses(n)
+            if late is not None:
+                for up, where, inside, on in ways(1):
+                    @pl.when((place == (depth - 1 if up else 0)) & jnp.logical_not(late))
+                    def _():
+                        for half in range(2):
+                            cross_copy(where, half, n).wait_send()
 
         def finish_text(s, carry):
             def one(n, c):
@@ -428,7 +524,7 @@
             lax.fori_loop(0, pieces, one, 0)
             return carry
 
-        lax.fori_loop(0, depth, finish_text, 0)
+        lax.fori_loop(1, depth, finish_text, 0)
 
         def finish_share(where, carry):
             lax.fori_loop(0, pieces, lambda n, c: (share_copy(where, core, n).wait_send(), c)[1], 0)
@@ -456,7 +552,7 @@
     pieces = 2 * PARTS
     return pl.pallas_call(
         functools.partial(kernel, tiles, relay_text),
-        out_shape=jax.ShapeDtypeStruct((tokens, width), bf16),
+        out_shape=pltpu.VMEM((tokens, width), bf16),
         in_specs=[smem] + [anywhere] * 7,
         out_specs=vmem,
         scratch_shapes=[
@@ -473,10 +569,12 @@
             pltpu.VMEM((tokens, width), f32),
             pltpu.VMEM((HEADS, tokens, text_total), bf16),
             dma((7,)),
-            dma((CHUNKS, PLANE - 1, 3)),
-            dma((CHUNKS, PLANE - 1, 3)),
-            dma((CHUNKS, 2, 2)),
-            dma((CHUNKS, 2, 2)),
+            dma((PAIRS, PLANE - 1, 2)),
+            dma((PAIRS, PLANE - 1, 2)),
+            dma((CHUNKS, PLANE - 1)),
+            dma((CHUNKS, PLANE - 1)),
+            dma((PAIRS, 2, 2)),
+            dma((PAIRS, 2, 2)),
             dma((CHUNKS, PLANE - 1)),
             dma((CHUNKS, PLANE - 1)),
             dma((pieces,)),
@@ -485,6 +583,8 @@
             dma((held, 2, pieces)),
             dma((held, pieces)),
             dma((held, pieces)),
+            dma((2, pieces)),
+            dma((2, pieces)),
         ],
         compiler_params=pltpu.CompilerParams(
             collective_id=0, has_side_effects=True, vmem_limit_bytes=60 * 1024 * 1024

time: 74.8 us -> 69.8 us (0.933)
  Pallas kernels: 71.7 us -> 68 us
  local copies, waits for them, and re-layouts: 2.29 us -> 0.97 us
    pallas_call x1, Pallas kernels: 71.7 us -> 68 us  [shards(): pl.pallas_call(functools.partial(kernel, tiles, relay_text), out_shape=pl...]
    unnamed x1, local copies, waits for them, and re-layouts: 2.29 us -> 0.97 us
where the time goes in v2:
time: 69.8 us; the launch traced here: 69.7 us
  Pallas kernels  68 us (97%)
  local copies, waits for them, and re-layouts  0.97 us (1%)
    pallas_call x1, Pallas kernels, shards(): pl.pallas_call(functools.partial(kernel, tiles, relay_text), out_shape=pl...  68 us

profile of v2, /device:TPU:0, one launch (start us, length us, event | category | flops | bytes accessed | tf_op | source)
XLA Modules:
  0.0 69.7 jit_solution(9845389091793439469)
XLA Ops:
  0.7 68.0 %shard_map.82 = bf16[128,4096]{1,0:T(8,128)(2,1)S(1)} custom-call(s32[1]{0:T(128)S(6)} %copy.11.step_ref, bf16[128,4096]{1,0:T(8,128)(2,1)} %q_hbm.1, bf16[128,4096]{1,0:T(8,128)(2,1)} %k_hbm.1, bf16[128,4096]{1,0:T(8,128)(2,1)} %v_hbm.1, bf16[128,4096]{1,0:T(8,128)(2,1)} %cq_hbm.1, bf16[16,4096]{1,0:T(8,128)(2,1)} %tk_hbm.1, bf16[16,4096]{1,0:T(8,128)(2,1)} %tv_hbm.1, ...), custom_call_target="tpu_custom_call" | custom-call | tf_op jit(solution)/shard_map/pallas_call | solution.py:553
  68.7 1.0 %copy.10 = bf16[128,4096]{1,0:T(8,128)(2,1)} copy(bf16[128,4096]{1,0:T(8,128)(2,1)S(1)} %shard_map.82) | data formatting | bytes 2097152

commit v3 on v2

--- a/solution.py
+++ b/solution.py
@@ -13,13 +13,13 @@
 PLANE = 4
 WINDOW = PLANE + 2 * RADIUS
 PAIRS = 4
-CHUNKS = 8
-PARTS = 2
-HALF_ROUNDS = (0, 1)
+CHUNKS = 4
+UNROLL = 4
+PIECES = ((0, 0, 4), (0, 4, 4), (1, 0, 4), (1, 4, 4))
+HALF_ROUNDS = (0, 0, 1, 1)
 FIRST_ROUNDS = (1, 1, 2, 2)
-SECOND_ROUNDS = (0, 0, 2, 2)
-UNROLL = 4
-CROSSING = ((2,), (3,))
+SECOND_ROUNDS = (0, 0, 1, 1)
+CROSSING = ((3,), (2,))
 MESH = pl.DeviceIdType.MESH
 
 
@@ -43,7 +43,7 @@
 
 def kernel(
     tiles, relay_text, step_ref, q_hbm, k_hbm, v_hbm, cq_hbm, tk_hbm, tv_hbm, gate_hbm, out_ref,
-    qbuf, kvbuf, tbuf, cq_ref, gate_ref, gate_row, o32, o16, precv, orecv, inv_ref, weight_ref,
+    qbuf, kvbuf, tbuf, cq_ref, gate_ref, gate_row, o32, o16, orecv, inv_ref, weight_ref,
     local_sem, pair_send, pair_recv, q_send, q_recv, halo_send, halo_recv, o_send, o_recv,
     half_send, half_recv, chain_send, chain_recv, share_send, share_recv, cross_send, cross_recv,
 ):
@@ -55,8 +55,9 @@
     heads = columns // head_dim
     depth = tiles // PLANE
     text_rows = tk_hbm.shape[0]
-    pieces = 2 * PARTS
-    piece_columns = width // PARTS
+    pieces = len(PIECES)
+    keys = [n for n in range(pieces) if PIECES[n][0] == 0]
+    values = [n for n in range(pieces) if PIECES[n][0] == 1]
     reach = RADIUS * tokens
 
     t = lax.axis_index("tile")
@@ -153,35 +154,37 @@
         device = me + other(m)
         span = cols(c * columns, columns)
         if m == 1:
-            source, target = o32.at[rows(device * tokens, tokens), span], precv.at[:, span]
+            source, target = o32.at[rows(device * tokens, tokens), span], o32.at[pl.ds(PLANE * tokens, tokens), span]
         else:
             source, target = o16.at[rows(device * tokens, tokens), span], orecv.at[m - 2, :, span]
         return remote(source, target, o_send.at[c, m - 1], o_recv.at[c, m - 1], t + other(m))
 
     def part_columns(n):
-        return cols((n % PARTS) * piece_columns, piece_columns)
+        return pl.ds(PIECES[n][1] * width // 8, PIECES[n][2] * width // 8)
 
     def half_copy(n, half):
-        i = n // PARTS
+        i = PIECES[n][0]
         return remote(
             texts[i].at[:, part_columns(n)], tbuf.at[i, text_half(place, half), part_columns(n)],
             half_send.at[n], half_recv.at[n], t + other(2),
         )
 
     def chain_copy(where, half, n, up):
-        part = tbuf.at[n // PARTS, text_half(where, half), part_columns(n)]
+        where_rows = text_pair(where, core) if half is None else text_half(where, half)
+        part = tbuf.at[PIECES[n][0], where_rows, part_columns(n)]
+        half = 0 if half is None else half
         return remote(
             part, part, chain_send.at[where, half, n, int(up)], chain_recv.at[where, half, n],
             t + (PLANE if up else -PLANE),
         )
 
     def share_copy(where, which, n):
-        part = tbuf.at[n // PARTS, text_pair(where, which), part_columns(n)]
+        part = tbuf.at[PIECES[n][0], text_pair(where, which), part_columns(n)]
         return remote(part, part, share_send.at[where, n], share_recv.at[where, n], t + other(1))
 
-    def cross_copy(where, half, n):
-        part = tbuf.at[n // PARTS, text_half(where, half), part_columns(n)]
-        return remote(part, part, cross_send.at[half, n], cross_recv.at[half, n], t + other(2))
+    def cross_copy(where, n):
+        part = tbuf.at[PIECES[n][0], text_pair(where, core), part_columns(n)]
+        return remote(part, part, cross_send.at[n], cross_recv.at[n], t + other(2))
 
     crossing = depth > 2
 
@@ -196,51 +199,46 @@
         for up, where, inside, on in ways(s):
             @pl.when(inside)
             def _():
-                for half in range(2):
-                    chain_copy(where, half, n, up).wait_recv()
-
-                    @pl.when(on)
-                    def _():
-                        chain_copy(where, half, n, up).start()
+                chain_copy(where, None, n, up).wait_recv()
+
+                @pl.when(on)
+                def _():
+                    chain_copy(where, None, n, up).start()
 
                 share_copy(where, core, n).start()
 
-    def text_steps(s, first, last):
-        lax.fori_loop(first, last, lambda n, c: (text_step(s, n), c)[1], 0)
+    def text_steps(n):
+        lax.fori_loop(3, depth, lambda s, c: (text_step(s, n), c)[1], 0)
 
     def first_step(n):
         late = crosses(n)
-        if late is None:
-            text_step(1, n)
-            return
         for up, where, inside, on in ways(1):
             end = place == (depth - 1 if up else 0)
 
-            @pl.when(inside & jnp.logical_not(end & late))
+            @pl.when(inside if late is None else inside & jnp.logical_not(end & late))
             def _():
                 for half in range(2):
                     chain_copy(where, half, n, up).wait_recv()
 
-                    @pl.when(on)
-                    def _():
-                        chain_copy(where, half, n, up).start()
-
+                @pl.when(on)
+                def _():
+                    chain_copy(where, None, n, up).start()
+
+                if late is not None:
                     @pl.when(end)
                     def _():
-                        cross_copy(where, half, n).start()
+                        cross_copy(where, n).start()
 
                 share_copy(where, core, n).start()
 
-    def crossed():
-        for n in range(pieces):
-            late = crosses(n)
-            if late is not None:
-                for up, where, inside, on in ways(1):
-                    @pl.when((place == (depth - 1 if up else 0)) & late)
-                    def _():
-                        for half in range(2):
-                            cross_copy(where, half, n).wait_recv()
-                        share_copy(where, core, n).start()
+    def crossed(n):
+        late = crosses(n)
+        if late is not None:
+            for up, where, inside, on in ways(1):
+                @pl.when((place == (depth - 1 if up else 0)) & late)
+                def _():
+                    cross_copy(where, n).wait_recv()
+                    share_copy(where, core, n).start()
 
     def first_on(n, up, on):
         late = crosses(n)
@@ -301,10 +299,9 @@
             first_chain(side, n)
     for c in range(1, PAIRS):
         if relay_text:
-            for j in range(2):
-                if HALF_ROUNDS[j] == c - 1:
-                    for n in range(j * PARTS, (j + 1) * PARTS):
-                        half_copy(n, side).start()
+            for n in range(pieces):
+                if HALF_ROUNDS[n] == c - 1:
+                    half_copy(n, side).start()
         send_pair(c)
     lax.fori_loop(0, CHUNKS, send_query, 0)
     for copy in copies if not relay_text else copies[:5]:
@@ -351,10 +348,14 @@
         weight_ref[h] = rounded
         inv_ref[:, span] = jnp.broadcast_to(1.0 / total, (tokens, head_dim))
 
-    def cross_values(h):
+    per = HEADS // PLANE
+
+    def cross_value(h):
         span = cols(h * head_dim, head_dim)
-        summed = jnp.dot(weight_ref[h], tbuf[1, :, span], preferred_element_type=jnp.float32)
-        inv_ref[:, span] = summed * inv_ref[:, span]
+        return inv_ref[:, span] * jnp.dot(weight_ref[h], tbuf[1, :, span], preferred_element_type=jnp.float32)
+
+    def keep_value(h):
+        inv_ref[:, cols(h * head_dim, head_dim)] = cross_value(h)
 
     def combine(c, m):
         span = cols((me + other(m)) * quarter + c * columns, columns)
@@ -362,10 +363,21 @@
         if m == 0:
             part = o32[rows(me * tokens, tokens), own]
         elif m == 1:
-            part = precv[:, own]
+            part = o32[pl.ds(PLANE * tokens, tokens), own]
         else:
             part = orecv[m - 2, :, own].astype(jnp.float32)
         out_ref[:, span] = (part + inv_ref[:, span]).astype(out_ref.dtype)
+
+    def over_heads(step, first, last):
+        def four(n, carry):
+            for j in range(UNROLL):
+                step(UNROLL * n + j)
+            return carry
+
+        lax.fori_loop(first // UNROLL, last // UNROLL, four, 0)
+
+    def piece_heads(n):
+        return PIECES[n][1] * HEADS // 8, (PIECES[n][1] + PIECES[n][2]) * HEADS // 8
 
     def forward(c):
         for i in range(2):
@@ -416,7 +428,7 @@
     def forward_round(r, carry):
         forward(r)
         if relay_text:
-            text_turns(r, [HALF_ROUNDS[n // PARTS] for n in range(pieces)], half_step)
+            text_turns(r, HALF_ROUNDS, half_step)
             if depth > 1:
                 text_turns(r, FIRST_ROUNDS, first_step)
         return carry
@@ -436,33 +448,30 @@
     lax.fori_loop(0, CHUNKS, compute_round, 0)
     give(CHUNKS - 1)
 
+    def settle(group):
+        if relay_text:
+            for n in group:
+                crossed(n)
+            for n in group:
+                text_steps(n)
+
+    def here(n):
+        if relay_text:
+            shared(n)
+
+    settle(keys)
     if relay_text:
-        lax.fori_loop(3, depth, lambda s, c: (text_steps(s, 0, PARTS), c)[1], 0)
-        for n in range(PARTS):
-            shared(n)
-
-    def scores_four(n, carry):
-        for j in range(UNROLL):
-            cross_scores(UNROLL * n + j)
-        return carry
-
-    lax.fori_loop(0, HEADS // UNROLL, scores_four, 0)
-
+        for n in values:
+            crossed(n)
+    for n in keys:
+        here(n)
+        over_heads(cross_scores, *piece_heads(n))
     if relay_text:
-        crossed()
-        lax.fori_loop(3, depth, lambda s, c: (text_steps(s, PARTS, pieces), c)[1], 0)
-
-    per = HEADS // PARTS // UNROLL
-
-    def values_four(n, carry):
-        for j in range(UNROLL):
-            cross_values(UNROLL * n + j)
-        return carry
-
-    for n in range(PARTS):
-        if relay_text:
-            shared(PARTS + n)
-        lax.fori_loop(n * per, (n + 1) * per, values_four, 0)
+        for n in values:
+            text_steps(n)
+    for n in values:
+        here(n)
+        over_heads(keep_value, *piece_heads(n))
 
     def combine_chunk(c, carry):
         for m in range(PLANE):
@@ -508,26 +517,22 @@
                 for up, where, inside, on in ways(1):
                     @pl.when((place == (depth - 1 if up else 0)) & jnp.logical_not(late))
                     def _():
-                        for half in range(2):
-                            cross_copy(where, half, n).wait_send()
+                        cross_copy(where, n).wait_send()
 
         def finish_text(s, carry):
-            def one(n, c):
-                for up, where, inside, on in ways(s):
-                    @pl.when(inside & on)
-                    def _():
-                        for half in range(2):
-                            chain_copy(where, half, n, up).wait_send()
-
-                return c
-
-            lax.fori_loop(0, pieces, one, 0)
+            for up, where, inside, on in ways(s):
+                @pl.when(inside & on)
+                def _():
+                    for n in range(pieces):
+                        chain_copy(where, None, n, up).wait_send()
+
             return carry
 
         lax.fori_loop(1, depth, finish_text, 0)
 
         def finish_share(where, carry):
-            lax.fori_loop(0, pieces, lambda n, c: (share_copy(where, core, n).wait_send(), c)[1], 0)
+            for n in range(pieces):
+                share_copy(where, core, n).wait_send()
             return carry
 
         lax.fori_loop(0, depth, finish_share, 0)
@@ -549,7 +554,7 @@
     dma = pltpu.SemaphoreType.DMA
     bf16, f32 = jnp.bfloat16, jnp.float32
     held = depth if relay_text else 1
-    pieces = 2 * PARTS
+    pieces = len(PIECES)
     return pl.pallas_call(
         functools.partial(kernel, tiles, relay_text),
         out_shape=pltpu.VMEM((tokens, width), bf16),
@@ -562,9 +567,8 @@
             pltpu.VMEM((tokens, width), bf16),
             pltpu.VMEM((gate_table.shape[0], quarter), bf16),
             pltpu.VMEM((1, quarter), f32),
-            pltpu.VMEM((PLANE * tokens, quarter), f32),
+            pltpu.VMEM(((PLANE + 1) * tokens, quarter), f32),
             pltpu.VMEM((PLANE * tokens, quarter), bf16),
-            pltpu.VMEM((tokens, quarter), f32),
             pltpu.VMEM((2, tokens, quarter), bf16),
             pltpu.VMEM((tokens, width), f32),
             pltpu.VMEM((HEADS, tokens, text_total), bf16),
@@ -583,8 +587,8 @@
             dma((held, 2, pieces)),
             dma((held, pieces)),
             dma((held, pieces)),
-            dma((2, pieces)),
-            dma((2, pieces)),
+            dma((pieces,)),
+            dma((pieces,)),
         ],
         compiler_params=pltpu.CompilerParams(
             collective_id=0, has_side_effects=True, vmem_limit_bytes=60 * 1024 * 1024

time: 69.8 us -> 67.1 us (0.961)
  Pallas kernels: 68 us -> 65.3 us
    pallas_call x1, Pallas kernels: 68 us -> 65.3 us  [shards(): pl.pallas_call(functools.partial(kernel, tiles, relay_text), out_shape=pl...]
where the time goes in v3:
time: 67.1 us; the launch traced here: 66.9 us
  Pallas kernels  65.3 us (97%)
  local copies, waits for them, and re-layouts  0.97 us (1%)
    pallas_call x1, Pallas kernels, shards(): pl.pallas_call(functools.partial(kernel, tiles, relay_text), out_shape=pl...  65.3 us

profile of v3, /device:TPU:0, one launch (start us, length us, event | category | flops | bytes accessed | tf_op | source)
XLA Modules:
  0.0 66.9 jit_solution(3646386262640916772)
XLA Ops:
  0.7 65.3 %shard_map.82 = bf16[128,4096]{1,0:T(8,128)(2,1)S(1)} custom-call(s32[1]{0:T(128)S(6)} %copy.11.step_ref, bf16[128,4096]{1,0:T(8,128)(2,1)} %q_hbm.1, bf16[128,4096]{1,0:T(8,128)(2,1)} %k_hbm.1, bf16[128,4096]{1,0:T(8,128)(2,1)} %v_hbm.1, bf16[128,4096]{1,0:T(8,128)(2,1)} %cq_hbm.1, bf16[16,4096]{1,0:T(8,128)(2,1)} %tk_hbm.1, bf16[16,4096]{1,0:T(8,128)(2,1)} %tv_hbm.1, ...), custom_call_target="tpu_custom_call" | custom-call | tf_op jit(solution)/shard_map/pallas_call | solution.py:558
  65.9 1.0 %copy.10 = bf16[128,4096]{1,0:T(8,128)(2,1)} copy(bf16[128,4096]{1,0:T(8,128)(2,1)S(1)} %shard_map.82) | data formatting | bytes 2097152

commit v4 on v3

--- a/solution.py
+++ b/solution.py
@@ -14,7 +14,7 @@
 WINDOW = PLANE + 2 * RADIUS
 PAIRS = 4
 CHUNKS = 4
-UNROLL = 4
+UNROLL = 16
 PIECES = ((0, 0, 4), (0, 4, 4), (1, 0, 4), (1, 4, 4))
 HALF_ROUNDS = (0, 0, 1, 1)
 FIRST_ROUNDS = (1, 1, 2, 2)
@@ -303,7 +303,7 @@
                 if HALF_ROUNDS[n] == c - 1:
                     half_copy(n, side).start()
         send_pair(c)
-    lax.fori_loop(0, CHUNKS, send_query, 0)
+    lax.fori_loop(0, 2, send_query, 0)
     for copy in copies if not relay_text else copies[:5]:
         copy.wait()
 
@@ -431,6 +431,11 @@
             text_turns(r, HALF_ROUNDS, half_step)
             if depth > 1:
                 text_turns(r, FIRST_ROUNDS, first_step)
+
+        @pl.when(r >= 2)
+        def _():
+            send_query(r, 0)
+
         return carry
 
     def compute_round(c, carry):
@@ -448,44 +453,9 @@
     lax.fori_loop(0, CHUNKS, compute_round, 0)
     give(CHUNKS - 1)
 
-    def settle(group):
-        if relay_text:
-            for n in group:
-                crossed(n)
-            for n in group:
-                text_steps(n)
-
-    def here(n):
-        if relay_text:
-            shared(n)
-
-    settle(keys)
-    if relay_text:
-        for n in values:
-            crossed(n)
-    for n in keys:
-        here(n)
-        over_heads(cross_scores, *piece_heads(n))
-    if relay_text:
-        for n in values:
-            text_steps(n)
-    for n in values:
-        here(n)
-        over_heads(keep_value, *piece_heads(n))
-
-    def combine_chunk(c, carry):
-        for m in range(PLANE):
-            if m:
-                o_copy(c, m).wait_recv()
-            combine(c, m)
-        return carry
-
-    lax.fori_loop(0, CHUNKS, combine_chunk, 0)
-
-    def finish(c, carry):
+    def finish_queries(c, carry):
         for m in (1, 2, 3):
             q_copy(c, m).wait_send()
-            o_copy(c, m).wait_send()
         return carry
 
     def finish_pair(c, carry):
@@ -498,27 +468,71 @@
                     halo_copy(c, up, i).wait_send()
         return carry
 
-    lax.fori_loop(0, CHUNKS, finish, 0)
-    lax.fori_loop(0, PAIRS, finish_pair, 0)
-
+    def early_finish():
+        lax.fori_loop(0, PAIRS, finish_pair, 0)
+        lax.fori_loop(0, CHUNKS, finish_queries, 0)
+        if relay_text:
+            for n in range(pieces):
+                half_copy(n, side).wait_send()
+
+            for n in range(pieces):
+                for up, on in ((True, has_up), (False, has_down)):
+                    @pl.when(first_on(n, up, on))
+                    def _():
+                        for half in range(2):
+                            chain_copy(place, half, n, up).wait_send()
+
+                late = crosses(n)
+                if late is not None:
+                    for up, where, inside, on in ways(1):
+                        @pl.when((place == (depth - 1 if up else 0)) & jnp.logical_not(late))
+                        def _():
+                            cross_copy(where, n).wait_send()
+
+
+    def settle(group):
+        if relay_text:
+            for n in group:
+                crossed(n)
+            for n in group:
+                text_steps(n)
+
+    def here(n):
+        if relay_text:
+            shared(n)
+
+    settle(keys)
     if relay_text:
-        for n in range(pieces):
-            half_copy(n, side).wait_send()
-
-        for n in range(pieces):
-            for up, on in ((True, has_up), (False, has_down)):
-                @pl.when(first_on(n, up, on))
-                def _():
-                    for half in range(2):
-                        chain_copy(place, half, n, up).wait_send()
-
-            late = crosses(n)
-            if late is not None:
-                for up, where, inside, on in ways(1):
-                    @pl.when((place == (depth - 1 if up else 0)) & jnp.logical_not(late))
-                    def _():
-                        cross_copy(where, n).wait_send()
-
+        for n in values:
+            crossed(n)
+    for n in keys:
+        here(n)
+        over_heads(cross_scores, *piece_heads(n))
+    early_finish()
+    if relay_text:
+        for n in values:
+            text_steps(n)
+    for n in values:
+        here(n)
+        over_heads(keep_value, *piece_heads(n))
+
+    def combine_chunk(c, carry):
+        for m in range(PLANE):
+            if m:
+                o_copy(c, m).wait_recv()
+            combine(c, m)
+        return carry
+
+    lax.fori_loop(0, CHUNKS, combine_chunk, 0)
+
+    def finish_outputs(c, carry):
+        for m in (1, 2, 3):
+            o_copy(c, m).wait_send()
+        return carry
+
+    lax.fori_loop(0, CHUNKS, finish_outputs, 0)
+
+    if relay_text:
         def finish_text(s, carry):
             for up, where, inside, on in ways(s):
                 @pl.when(inside & on)

time: 67.1 us -> 66.2 us (0.987)
  Pallas kernels: 65.3 us -> 64.4 us
    pallas_call x1, Pallas kernels: 65.3 us -> 64.4 us  [shards(): pl.pallas_call(functools.partial(kernel, tiles, relay_text), out_shape=pl...]
where the time goes in v4:
time: 66.2 us; the launch traced here: 66 us
  Pallas kernels  64.4 us (97%)
  local copies, waits for them, and re-layouts  0.97 us (1%)
    pallas_call x1, Pallas kernels, shards(): pl.pallas_call(functools.partial(kernel, tiles, relay_text), out_shape=pl...  64.4 us

profile of v4, /device:TPU:0, one launch (start us, length us, event | category | flops | bytes accessed | tf_op | source)
XLA Modules:
  0.0 66.0 jit_solution(8955809823351405894)
XLA Ops:
  0.7 64.4 %shard_map.82 = bf16[128,4096]{1,0:T(8,128)(2,1)S(1)} custom-call(s32[1]{0:T(128)S(6)} %copy.11.step_ref, bf16[128,4096]{1,0:T(8,128)(2,1)} %q_hbm.1, bf16[128,4096]{1,0:T(8,128)(2,1)} %k_hbm.1, bf16[128,4096]{1,0:T(8,128)(2,1)} %v_hbm.1, bf16[128,4096]{1,0:T(8,128)(2,1)} %cq_hbm.1, bf16[16,4096]{1,0:T(8,128)(2,1)} %tk_hbm.1, bf16[16,4096]{1,0:T(8,128)(2,1)} %tv_hbm.1, ...), custom_call_target="tpu_custom_call" | custom-call | tf_op jit(solution)/shard_map/pallas_call | solution.py:572
  65.1 1.0 %copy.10 = bf16[128,4096]{1,0:T(8,128)(2,1)} copy(bf16[128,4096]{1,0:T(8,128)(2,1)S(1)} %shard_map.82) | data formatting | bytes 2097152

commit v5 on v4

--- a/solution.py
+++ b/solution.py
@@ -282,21 +282,23 @@
 
     def send_pair(c):
         for i in range(2):
-            for m in (2, 3, 1):
+            for m in (3, 2, 1):
                 pair_copy(c, m, i).start()
 
     def send_query(c, carry):
-        for m in (2, 3, 1):
+        for m in (3, 2, 1):
             q_copy(c, m).start()
         return carry
 
     copies = local_copies()
-    send_pair(0)
+    if not relay_text:
+        send_pair(0)
     if relay_text:
         for copy in copies[5:]:
             copy.wait()
         for n in range(pieces):
             first_chain(side, n)
+        send_pair(0)
     for c in range(1, PAIRS):
         if relay_text:
             for n in range(pieces):
@@ -409,7 +411,7 @@
                 self_head(c * heads + k, i)
 
     def give(c):
-        for m in (2, 3, 1):
+        for m in (3, 2, 1):
             o_copy(c, m).start()
 
     def text_turns(r, row, step):

time: 66.2 us -> 66.1 us (level)
  no operation moved by 1% of the time
where the time goes in v5:
time: 66.1 us; the launch traced here: 65.6 us
  Pallas kernels  63.9 us (97%)
  local copies, waits for them, and re-layouts  0.97 us (1%)
    pallas_call x1, Pallas kernels, shards(): pl.pallas_call(functools.partial(kernel, tiles, relay_text), out_shape=pl...  63.9 us

profile of v5, /device:TPU:0, one launch (start us, length us, event | category | flops | bytes accessed | tf_op | source)
XLA Modules:
  0.0 65.6 jit_solution(7286937112634537543)
XLA Ops:
  0.7 63.9 %shard_map.82 = bf16[128,4096]{1,0:T(8,128)(2,1)S(1)} custom-call(s32[1]{0:T(128)S(6)} %copy.11.step_ref, bf16[128,4096]{1,0:T(8,128)(2,1)} %q_hbm.1, bf16[128,4096]{1,0:T(8,128)(2,1)} %k_hbm.1, bf16[128,4096]{1,0:T(8,128)(2,1)} %v_hbm.1, bf16[128,4096]{1,0:T(8,128)(2,1)} %cq_hbm.1, bf16[16,4096]{1,0:T(8,128)(2,1)} %tk_hbm.1, bf16[16,4096]{1,0:T(8,128)(2,1)} %tv_hbm.1, ...), custom_call_target="tpu_custom_call" | custom-call | tf_op jit(solution)/shard_map/pallas_call | solution.py:574
  64.6 1.0 %copy.10 = bf16[128,4096]{1,0:T(8,128)(2,1)} copy(bf16[128,4096]{1,0:T(8,128)(2,1)S(1)} %shard_map.82) | data formatting | bytes 2097152

commit v6 on v5

--- a/solution.py
+++ b/solution.py
@@ -525,7 +525,8 @@
             combine(c, m)
         return carry
 
-    lax.fori_loop(0, CHUNKS, combine_chunk, 0)
+    for c in range(CHUNKS):
+        combine_chunk(c, 0)
 
     def finish_outputs(c, carry):
         for m in (1, 2, 3):

time: 66.1 us -> 66.1 us (level)
  no operation moved by 1% of the time
where the time goes in v6:
time: 66.1 us; the launch traced here: 65.6 us
  Pallas kernels  63.9 us (97%)
  local copies, waits for them, and re-layouts  0.97 us (1%)
    pallas_call x1, Pallas kernels, shards(): pl.pallas_call(functools.partial(kernel, tiles, relay_text), out_shape=pl...  63.9 us

profile of v6, /device:TPU:0, one launch (start us, length us, event | category | flops | bytes accessed | tf_op | source)
XLA Modules:
  0.0 65.6 jit_solution(15830795653392944194)
XLA Ops:
  0.7 63.9 %shard_map.82 = bf16[128,4096]{1,0:T(8,128)(2,1)S(1)} custom-call(s32[1]{0:T(128)S(6)} %copy.11.step_ref, bf16[128,4096]{1,0:T(8,128)(2,1)} %q_hbm.1, bf16[128,4096]{1,0:T(8,128)(2,1)} %k_hbm.1, bf16[128,4096]{1,0:T(8,128)(2,1)} %v_hbm.1, bf16[128,4096]{1,0:T(8,128)(2,1)} %cq_hbm.1, bf16[16,4096]{1,0:T(8,128)(2,1)} %tk_hbm.1, bf16[16,4096]{1,0:T(8,128)(2,1)} %tv_hbm.1, ...), custom_call_target="tpu_custom_call" | custom-call | tf_op jit(solution)/shard_map/pallas_call | solution.py:575
  64.6 1.0 %copy.10 = bf16[128,4096]{1,0:T(8,128)(2,1)} copy(bf16[128,4096]{1,0:T(8,128)(2,1)S(1)} %shard_map.82) | data formatting | bytes 2097152
